TPU v7x, 32 devices: a whole 2x2x4 slice. The times are simulated.
32 devices in a mesh: section: 2 (over x), dp: 4 (over z), mp: 4 (over y, core).
Axes of the slice: x: 2, y: 2, z: 4, core: 2. Of those that a mesh axis runs over, the one named last changes fastest.
Arguments:
- text_feats: bfloat16 [4096, 512], P('dp'), may hold values from -48 to 48
- image_feats: bfloat16 [4096, 512], P(('dp', 'mp')), may hold values from -48 to 48
- logit_scale: float32 [1], replicated, may hold values from 10 to 320
- layer_inputs: bfloat16 [2, 4096, 512], P('section', 'dp'), may hold values from -6 to 6
- w_in: bfloat16 [2, 512, 2048], P('section', None, 'mp'), may hold values from -0.25 to 0.25
- w_out: bfloat16 [2, 2048, 512], P('section', 'mp'), may hold values from -0.125 to 0.125
Outputs:
- image_grad: bfloat16 [4096, 512], P(('dp', 'mp'))
- input_grad: bfloat16 [4096, 512], P('dp', 'section')
- w_in_grad: float32 [2, 512, 2048], P('section', 'dp', 'mp')
- w_out_grad_t: float32 [2, 512, 2048], P('section', 'dp', 'mp')
All inputs are finite; a program needn't handle non-finite values.
Results may differ from a plain program's by a relative error of at most 0.017.
Values may be sent and summed in bfloat16 or wider, within the bound.
A program may use at most 128 MiB of HBM per device.

v0:
```python
import jax
import jax.numpy as jnp
from jax import lax
from jax.sharding import PartitionSpec as P

MICRO = 4


def shifted(block, axis, distance):
    devices = range(lax.axis_size(axis))
    route = [(i - distance, i) for i in devices if i - distance in devices]
    return lax.ppermute(block, axis, route)


def spread(value, axis, source):
    kept = jnp.where(lax.axis_index(axis) == source, value, 0).astype(value.dtype)
    return lax.psum(kept, axis)


def unit_rows(values):
    wide = values.astype(jnp.float32)
    length = jnp.sqrt(jnp.sum(wide * wide, axis=1, keepdims=True) + 1.0)
    return (wide / length, length)


def unit_backward(unit, length, grad_unit):
    return (grad_unit - unit * jnp.sum(unit * grad_unit, axis=1, keepdims=True)) / length


def quick_gelu(values):
    return values * jax.nn.sigmoid(1.702 * values)


def quick_slope(values):
    sigm = jax.nn.sigmoid(1.702 * values)
    return sigm + 1.702 * values * sigm * (1.0 - sigm)


def contract_rows(left_side, right_side):
    return lax.dot_general(
        left_side, right_side, (((0,), (0,)), ((), ())), preferred_element_type=jnp.float32
    )


def contract_cols(left_side, right_side):
    return lax.dot_general(
        left_side, right_side, (((1,), (1,)), ((), ())), preferred_element_type=jnp.float32
    )


def body(text_feats, image_feats, logit_scale, layer_inputs, w_in, w_out):
    logit_mult = logit_scale[0]
    mp_count = lax.axis_size("mp")
    segment_count = lax.axis_size("section")
    dp_index = lax.axis_index("dp")
    mp_index = lax.axis_index("mp")
    segment_index = lax.axis_index("section")
    row_count = text_feats.shape[0]
    own_rows = image_feats.shape[0]
    text_unit, text_length = unit_rows(text_feats)
    image_unit, image_length = unit_rows(image_feats)
    text_low = text_unit.astype(jnp.bfloat16)
    image_low = image_unit.astype(jnp.bfloat16)
    columns = lax.all_gather(image_low, "dp", axis=0, tiled=True)
    column_total_count = columns.shape[0]
    scores = logit_mult * contract_cols(text_low, columns)
    text_ids = dp_index * row_count + jnp.arange(row_count, dtype=jnp.int32)
    column_pos = jnp.arange(column_total_count, dtype=jnp.int32)
    image_ids = (column_pos // own_rows * mp_count + mp_index) * own_rows + column_pos % own_rows
    positive = (text_ids[:, None] == image_ids[None, :]).astype(jnp.float32)
    row_peak = lax.pmax(jnp.max(scores, axis=1), "mp")
    column_peak = lax.pmax(jnp.max(scores, axis=0), "dp")
    row_total = lax.psum(jnp.sum(jnp.exp(scores - row_peak[:, None]), axis=1), "mp")
    column_local = jnp.sum(jnp.exp(scores - column_peak[None, :]), axis=0)
    column_total = lax.psum(column_local, "dp")
    row_prob = jnp.exp(scores - row_peak[:, None]) / row_total[:, None]
    column_prob = jnp.exp(scores - column_peak[None, :]) / column_total[None, :]
    score_grad = (0.5 * (row_prob + column_prob) - positive).astype(jnp.bfloat16)
    text_share = logit_mult * jnp.dot(score_grad, columns, preferred_element_type=jnp.float32)
    text_unit_grad = lax.psum(text_share, "mp")
    top_grad = unit_backward(text_unit, text_length, text_unit_grad).astype(jnp.bfloat16)
    image_unit_grad = lax.psum_scatter(
        (logit_mult * contract_rows(score_grad, text_low)).astype(jnp.bfloat16),
        "dp",
        scatter_dimension=0,
        tiled=True,
    ).astype(jnp.float32)
    image_grad = unit_backward(image_unit, image_length, image_unit_grad).astype(jnp.bfloat16)
    segment_inputs = layer_inputs[0]
    w_first = w_in[0]
    w_second = w_out[0]
    step_rows = row_count // MICRO
    last_segment = segment_count - 1
    time_steps = MICRO + segment_count - 1
    is_last = segment_index == last_segment
    is_first = segment_index == 0
    incoming = jnp.zeros((step_rows, segment_inputs.shape[1]), jnp.bfloat16)
    grad_first = jnp.zeros(w_first.shape, jnp.float32)
    grad_second = jnp.zeros(w_first.shape, jnp.float32)
    finished = jnp.zeros((row_count, segment_inputs.shape[1]), jnp.bfloat16)
    for time_step in range(time_steps):
        micro_slot = time_step - last_segment + segment_index
        active = jnp.logical_and(micro_slot >= 0, micro_slot < MICRO)
        row_start = jnp.clip(micro_slot, 0, MICRO - 1) * step_rows
        top_start = min(time_step, MICRO - 1) * step_rows
        top_piece = top_grad[top_start : top_start + step_rows]
        grad_now = jnp.where(is_last, top_piece, incoming)
        inputs_now = lax.dynamic_slice_in_dim(segment_inputs, row_start, step_rows, 0)
        pre_act = jnp.dot(inputs_now, w_first, preferred_element_type=jnp.float32)
        activation = quick_gelu(pre_act).astype(jnp.bfloat16)
        back_grad = contract_cols(grad_now, w_second)
        pre_grad = (back_grad * quick_slope(pre_act)).astype(jnp.bfloat16)
        unit_share = contract_cols(pre_grad, w_first)
        summed = lax.psum(unit_share.astype(jnp.bfloat16), "mp").astype(jnp.float32)
        grad_prev = (grad_now.astype(jnp.float32) + summed).astype(jnp.bfloat16)
        weight = active.astype(jnp.float32)
        grad_first = grad_first + weight * contract_rows(inputs_now, pre_grad)
        grad_second = grad_second + weight * contract_rows(grad_now, activation)
        updated = lax.dynamic_update_slice_in_dim(finished, grad_prev, row_start, 0)
        finished = jnp.where(jnp.logical_and(active, is_first), updated, finished)
        if time_step + 1 < time_steps:
            incoming = shifted(grad_prev, "section", -1)
    whole_grad = spread(finished, "section", 0)
    feature_width = whole_grad.shape[1] // segment_count
    feature_start = segment_index * feature_width
    input_grad = lax.dynamic_slice_in_dim(whole_grad, feature_start, feature_width, 1)
    first_sum, second_sum = (
        lax.psum_scatter(
            grad_first.astype(jnp.bfloat16), "dp", scatter_dimension=0, tiled=True
        ).astype(jnp.float32),
        lax.psum_scatter(
            grad_second.astype(jnp.bfloat16), "dp", scatter_dimension=0, tiled=True
        ).astype(jnp.float32),
    )
    return (image_grad, input_grad, first_sum[None], second_sum[None])


def solution(mesh):
    placed = (
        P("dp", None),
        P(("dp", "mp"), None),
        P(),
        P("section", "dp", None),
        P("section", None, "mp"),
        P("section", "mp", None),
    )
    return jax.shard_map(
        body,
        mesh=mesh,
        in_specs=placed,
        out_specs=(
            P(("dp", "mp"), None),
            P("dp", "section"),
            P("section", "dp", "mp"),
            P("section", "dp", "mp"),
        ),
        check_vma=False,
    )
```

profile of v0, /device:TPU:0, one launch (start us, length us, event | category | flops | bytes accessed | tf_op | source)
XLA Modules:
  0.0 491.8 jit_solution(6473197469235849443)
XLA Ops:
  12.5 28.6 %all-gather.2.cloned.1.call-done = bf16[1024,512]{1,0:T(8,128)(2,1)} async-done(((bf16[256,512]{1,0:T(8,128)(2,1)}), bf16[1024,512]{1,0:T(8,128)(2,1)}) %all-gather.2.cloned.1.call-update) | async-done | bytes 1048592 | tf_op jit(solution)/shard_map/all_gather | solution.py:64
  41.1 4.5 multiply_reduce_fusion.1
  45.7 6.0 %pmax.14 = f32[1024]{0:T(1024)S(1)} all-reduce(f32[1024]{0:T(1024)S(1)} %get-tuple-element.14), channel_id=1, replica_groups=mesh['section'=2,'dp'=4,'mp'=4] {'mp'}, use_global_device_ids=true, to_apply=%region_3.4 | all-reduce | flops 1024 | bytes 8192 | tf_op jit(solution)/shard_map/pmax | solution.py:71
  51.7 3.2 fusion
  54.9 10.9 %pmax.15 = f32[1024]{0:T(1024)S(1)} all-reduce(f32[1024]{0:T(1024)S(1)} %get-tuple-element.5), channel_id=1, replica_groups=mesh['section'=2,'dp'=4,'mp'=4] {'dp'}, use_global_device_ids=true, to_apply=%region_7.8 | all-reduce | flops 1024 | bytes 8192 | tf_op jit(solution)/shard_map/pmax | solution.py:72
  65.8 2.9 fusion.1
  68.7 8.4 %psum.64 = f32[1024]{0:T(1024)S(1)} all-reduce(f32[1024]{0:T(1024)S(1)} %fusion.1), channel_id=1, replica_groups=mesh['section'=2,'dp'=4,'mp'=4] {'dp'}, use_global_device_ids=true, to_apply=%region_9.10 | all-reduce | flops 1024 | bytes 8192 | tf_op jit(solution)/shard_map/psum | solution.py:75
  77.1 5.7 %psum.63 = f32[1024]{0:T(1024)S(1)} all-reduce(f32[1024]{0:T(1024)S(1)} %get-tuple-element.4), channel_id=1, replica_groups=mesh['section'=2,'dp'=4,'mp'=4] {'mp'}, use_global_device_ids=true, to_apply=%region_5.6 | all-reduce | flops 1024 | bytes 8192 | tf_op jit(solution)/shard_map/psum | solution.py:73
  82.8 3.9 subtract_convert_fusion
  92.0 49.2 %all-reduce.8.cloned.1.call-done = f32[1024,512]{1,0:T(8,128)} async-done(((f32[1024,512]{1,0:T(8,128)}), f32[1024,512]{1,0:T(8,128)}) %all-reduce.8.cloned.1.call-update) | async-done | bytes 2097168 | tf_op jit(solution)/shard_map/psum | solution.py:80
  147.1 32.5 %all-reduce.10.cloned.1.call-done = bf16[256,512]{1,0:T(8,128)(2,1)} async-done(((bf16[256,512]{1,0:T(8,128)(2,1)}), bf16[256,512]{1,0:T(8,128)(2,1)}) %all-reduce.10.cloned.1.call-update) | async-done | bytes 262160 | tf_op jit(solution)/shard_map/psum | solution.py:114
  184.0 6.8 %collective-permute-done = bf16[256,512]{1,0:T(8,128)(2,1)S(1)} collective-permute-done((bf16[256,512]{1,0:T(8,128)(2,1)S(1)}, bf16[256,512]{1,0:T(8,128)(2,1)S(1)}, u32[]{:S(2)}, u32[]{:S(2)}) %collective-permute-start) | collective-permute-done | bytes 262176 | tf_op jit(solution)/shard_map/ppermute | solution.py:12
  194.1 32.4 %all-reduce.12.cloned.1.call-done = bf16[256,512]{1,0:T(8,128)(2,1)} async-done(((bf16[256,512]{1,0:T(8,128)(2,1)}), bf16[256,512]{1,0:T(8,128)(2,1)}) %all-reduce.12.cloned.1.call-update) | async-done | bytes 262160 | tf_op jit(solution)/shard_map/psum | solution.py:114
  229.9 6.9 %collective-permute-done.1 = bf16[256,512]{1,0:T(8,128)(2,1)} collective-permute-done((bf16[256,512]{1,0:T(8,128)(2,1)S(1)}, bf16[256,512]{1,0:T(8,128)(2,1)}, u32[]{:S(2)}, u32[]{:S(2)}) %collective-permute-start.1) | collective-permute-done | bytes 262176 | tf_op jit(solution)/shard_map/ppermute | solution.py:12
  241.1 32.4 %all-reduce.14.cloned.1.call-done = bf16[256,512]{1,0:T(8,128)(2,1)} async-done(((bf16[256,512]{1,0:T(8,128)(2,1)}), bf16[256,512]{1,0:T(8,128)(2,1)}) %all-reduce.14.cloned.1.call-update) | async-done | bytes 262160 | tf_op jit(solution)/shard_map/psum | solution.py:114
  277.0 7.1 %collective-permute-done.2 = bf16[256,512]{1,0:T(8,128)(2,1)} collective-permute-done((bf16[256,512]{1,0:T(8,128)(2,1)}, bf16[256,512]{1,0:T(8,128)(2,1)}, u32[]{:S(2)}, u32[]{:S(2)}) %collective-permute-start.2) | collective-permute-done | bytes 262176 | tf_op jit(solution)/shard_map/ppermute | solution.py:12
  288.1 32.4 %all-reduce.16.cloned.1.call-done = bf16[256,512]{1,0:T(8,128)(2,1)} async-done(((bf16[256,512]{1,0:T(8,128)(2,1)}), bf16[256,512]{1,0:T(8,128)(2,1)}) %all-reduce.16.cloned.1.call-update) | async-done | bytes 262160 | tf_op jit(solution)/shard_map/psum | solution.py:114
  324.3 6.9 %collective-permute-done.3 = bf16[256,512]{1,0:T(8,128)(2,1)} collective-permute-done((bf16[256,512]{1,0:T(8,128)(2,1)}, bf16[256,512]{1,0:T(8,128)(2,1)}, u32[]{:S(2)}, u32[]{:S(2)}) %collective-permute-start.3) | collective-permute-done | bytes 262176 | tf_op jit(solution)/shard_map/ppermute | solution.py:12
  335.2 4.0 multiply_convert_fusion
  350.5 17.1 %all-reduce.18.cloned.1.call-done = bf16[256,512]{1,0:T(8,128)(2,1)} async-done(((bf16[256,512]{1,0:T(8,128)(2,1)}), bf16[256,512]{1,0:T(8,128)(2,1)}) %all-reduce.18.cloned.1.call-update) | async-done | bytes 262160 | tf_op jit(solution)/shard_map/psum | solution.py:114
  371.8 25.4 %reduce-scatter.4.cloned.1.call-done = bf16[256,512]{1,0:T(8,128)(2,1)} async-done(((bf16[1024,512]{1,0:T(8,128)(2,1)}), bf16[256,512]{1,0:T(8,128)(2,1)}) %reduce-scatter.4.cloned.1.call-update) | async-done | bytes 262160 | tf_op jit(solution)/shard_map/reduce_scatter | solution.py:82
  400.2 20.2 %reduce-scatter.6.cloned.1.call-done = bf16[128,512]{1,0:T(8,128)(2,1)} async-done(((bf16[512,512]{1,0:T(8,128)(2,1)}), bf16[128,512]{1,0:T(8,128)(2,1)}) %reduce-scatter.6.cloned.1.call-update) | async-done | bytes 131088 | tf_op jit(solution)/shard_map/reduce_scatter | solution.py:128
  422.1 20.6 %reduce-scatter.8.cloned.1.call-done = bf16[128,512]{1,0:T(8,128)(2,1)} async-done(((bf16[512,512]{1,0:T(8,128)(2,1)}), bf16[128,512]{1,0:T(8,128)(2,1)}) %reduce-scatter.8.cloned.1.call-update) | async-done | bytes 131088 | tf_op jit(solution)/shard_map/reduce_scatter | solution.py:131
  444.3 39.1 %all-reduce.20.cloned.1.call-done = bf16[1024,512]{1,0:T(8,128)(2,1)} async-done(((bf16[1024,512]{1,0:T(8,128)(2,1)}), bf16[1024,512]{1,0:T(8,128)(2,1)}) %all-reduce.20.cloned.1.call-update) | async-done | bytes 1048592 | tf_op jit(solution)/shard_map/psum | solution.py:17
  (142 shorter events, 69.7 us)
Async XLA Ops:
  7.2 83.5 %copy-start = (bf16[1,1024,512]{2,1,0:T(8,128)(2,1)S(1)}, bf16[1,1024,512]{2,1,0:T(8,128)(2,1)}, u32[]{:S(2)}) copy-start(bf16[1,1024,512]{2,1,0:T(8,128)(2,1)} %param.9) | copy-start | bytes 3145732
  7.2 34.0 %copy-start.2 = (bf16[1024,512]{1,0:T(8,128)(2,1)S(1)}, bf16[1024,512]{1,0:T(8,128)(2,1)}, u32[]{:S(2)}) copy-start(bf16[1024,512]{1,0:T(8,128)(2,1)} %param.6) | copy-start | bytes 3145732
  7.2 33.9 %all-gather.2.cloned.1.call-start = ((), (), s32[]{:S(2)}) async-start(), calls=%async_computation.3 | async-start | bytes 1310720 | tf_op jit(solution)/shard_map/all_gather | solution.py:64
  10.3 130.9 %all-reduce.8.cloned.1.call-start = ((), (), s32[]{:S(2)}) async-start(), calls=%async_computation.5 | async-start | bytes 4194304 | tf_op jit(solution)/shard_map/psum | solution.py:80
  90.6 88.9 %all-reduce.10.cloned.1.call-start = ((), (), s32[]{:S(2)}) async-start(), calls=%async_computation.6 | async-start | bytes 524288 | tf_op jit(solution)/shard_map/psum | solution.py:114
  92.0 51.9 %copy-start.23 = (f32[256,512]{1,0:T(8,128)}, f32[256,512]{1,0:T(8,128)S(1)}, u32[]{:S(2)}) copy-start(f32[256,512]{1,0:T(8,128)S(1)} %fusion.35) | copy-start | bytes 1572868
  147.0 79.4 %all-reduce.12.cloned.1.call-start = ((), (), s32[]{:S(2)}) async-start(), calls=%async_computation.7 | async-start | bytes 524288 | tf_op jit(solution)/shard_map/psum | solution.py:114
  182.4 8.4 %collective-permute-start = (bf16[256,512]{1,0:T(8,128)(2,1)S(1)}, bf16[256,512]{1,0:T(8,128)(2,1)S(1)}, u32[]{:S(2)}, u32[]{:S(2)}) collective-permute-start(bf16[256,512]{1,0:T(8,128)(2,1)S(1)} %get-tuple-element.13), channel_id=1, source_target_pairs={{16,0},{17,1},{18,2},{19,3},{20,4},{21,5},{22,6},{23,7},{24,8},{25... | collective-permute-start | bytes 786440 | tf_op jit(solution)/shard_map/ppermute | solution.py:12
  191.8 34.6 %copy-start.17 = (bf16[256,512]{1,0:T(8,128)(2,1)}, bf16[256,512]{1,0:T(8,128)(2,1)S(1)}, u32[]{:S(2)}) copy-start(bf16[256,512]{1,0:T(8,128)(2,1)S(1)} %slice_select_fusion.1) | copy-start | bytes 786436
  194.0 79.5 %all-reduce.14.cloned.1.call-start = ((), (), s32[]{:S(2)}) async-start(), calls=%async_computation.8 | async-start | bytes 524288 | tf_op jit(solution)/shard_map/psum | solution.py:114
  228.3 8.5 %collective-permute-start.1 = (bf16[256,512]{1,0:T(8,128)(2,1)S(1)}, bf16[256,512]{1,0:T(8,128)(2,1)}, u32[]{:S(2)}, u32[]{:S(2)}) collective-permute-start(bf16[256,512]{1,0:T(8,128)(2,1)S(1)} %get-tuple-element.11), channel_id=1, source_target_pairs={{16,0},{17,1},{18,2},{19,3},{20,4},{21,5},{22,6},{23,7},{24,8},{25... | collective-permute-start | bytes 786440 | tf_op jit(solution)/shard_map/ppermute | solution.py:12
  241.0 79.5 %all-reduce.16.cloned.1.call-start = ((), (), s32[]{:S(2)}) async-start(), calls=%async_computation.9 | async-start | bytes 524288 | tf_op jit(solution)/shard_map/psum | solution.py:114
  275.4 8.7 %collective-permute-start.2 = (bf16[256,512]{1,0:T(8,128)(2,1)}, bf16[256,512]{1,0:T(8,128)(2,1)}, u32[]{:S(2)}, u32[]{:S(2)}) collective-permute-start(bf16[256,512]{1,0:T(8,128)(2,1)} %get-tuple-element.9), channel_id=1, source_target_pairs={{16,0},{17,1},{18,2},{19,3},{20,4},{21,5},{22,6},{23,7},{24,8},{25... | collective-permute-start | bytes 786440 | tf_op jit(solution)/shard_map/ppermute | solution.py:12
  276.7 9.2 %copy-start.31 = (bf16[1,512,512]{2,1,0:T(8,128)(2,1)S(1)}, bf16[1,512,512]{2,1,0:T(8,128)(2,1)}, u32[]{:S(2)}) copy-start(bf16[1,512,512]{2,1,0:T(8,128)(2,1)} %param.11) | copy-start | bytes 1572868
  277.0 9.3 %copy-start.25 = (f32[256,512]{1,0:T(8,128)}, f32[256,512]{1,0:T(8,128)S(1)}, u32[]{:S(2)}) copy-start(f32[256,512]{1,0:T(8,128)S(1)} %fusion.26) | copy-start | bytes 1572868
  288.1 79.5 %all-reduce.18.cloned.1.call-start = ((), (), s32[]{:S(2)}) async-start(), calls=%async_computation.10 | async-start | bytes 524288 | tf_op jit(solution)/shard_map/psum | solution.py:114
  322.5 8.7 %collective-permute-start.3 = (bf16[256,512]{1,0:T(8,128)(2,1)}, bf16[256,512]{1,0:T(8,128)(2,1)}, u32[]{:S(2)}, u32[]{:S(2)}) collective-permute-start(bf16[256,512]{1,0:T(8,128)(2,1)} %get-tuple-element.7), channel_id=1, source_target_pairs={{16,0},{17,1},{18,2},{19,3},{20,4},{21,5},{22,6},{23,7},{24,8},{25... | collective-permute-start | bytes 786440 | tf_op jit(solution)/shard_map/ppermute | solution.py:12
  324.0 9.0 %copy-start.32 = (bf16[1,512,512]{2,1,0:T(8,128)(2,1)S(1)}, bf16[1,512,512]{2,1,0:T(8,128)(2,1)}, u32[]{:S(2)}) copy-start(bf16[1,512,512]{2,1,0:T(8,128)(2,1)} %param.11) | copy-start | bytes 1572868
  324.3 9.1 %copy-start.26 = (f32[256,512]{1,0:T(8,128)}, f32[256,512]{1,0:T(8,128)S(1)}, u32[]{:S(2)}) copy-start(f32[256,512]{1,0:T(8,128)S(1)} %fusion.23) | copy-start | bytes 1572868
  335.2 62.0 %reduce-scatter.4.cloned.1.call-start = ((), (), s32[]{:S(2)}) async-start(), calls=%async_computation.4 | async-start | bytes 1310720 | tf_op jit(solution)/shard_map/reduce_scatter | solution.py:82
  339.2 81.2 %reduce-scatter.6.cloned.1.call-start = ((), (), s32[]{:S(2)}) async-start(), calls=%async_computation.12 | async-start | bytes 655360 | tf_op jit(solution)/shard_map/reduce_scatter | solution.py:128
  345.3 97.4 %reduce-scatter.8.cloned.1.call-start = ((), (), s32[]{:S(2)}) async-start(), calls=%async_computation.13 | async-start | bytes 655360 | tf_op jit(solution)/shard_map/reduce_scatter | solution.py:131
  350.5 132.9 %all-reduce.20.cloned.1.call-start = ((), (), s32[]{:S(2)}) async-start(), calls=%async_computation.11 | async-start | bytes 2097152 | tf_op jit(solution)/shard_map/psum | solution.py:17
  367.6 29.6 %copy-start.5 = (bf16[256,512]{1,0:T(8,128)(2,1)S(1)}, bf16[256,512]{1,0:T(8,128)(2,1)}, u32[]{:S(2)}) copy-start(bf16[256,512]{1,0:T(8,128)(2,1)} %param.7) | copy-start | bytes 786436
  (24 other events, 50.3 us)
Sparse Core Ops, SparseCore 0:
  10.4 30.6 all-gather.1
  90.8 50.3 all-reduce.7
  147.2 32.3 all-reduce.9
  194.1 32.2 all-reduce.11
  241.1 32.2 all-reduce.13
  288.2 32.2 all-reduce.15
  335.3 32.2 all-reduce.17
  369.9 27.2 reduce-scatter.3
  400.1 20.3 reduce-scatter.5
  422.5 20.0 reduce-scatter.7
  445.0 38.3 all-reduce.19
where the time goes:
time: 493 us; the launch traced here: 492 us
  waiting for transfers between devices  358 us (73%)
  other arithmetic  39.4 us (8%)
  blocking collectives  31 us (6%)
  matrix products  30.8 us (6%)
  between operations  15.1 us (3%)
  local copies, waits for them, and re-layouts  12.1 us (2%)
  starting transfers between devices  5.75 us (1%)
    psum x5, waiting for transfers between devices, body(): summed = lax.psum(unit_share.astype(jnp.bfloat16), 'mp').astype(jnp.float32)  147 us
    psum x1, waiting for transfers between devices, body(): text_unit_grad = lax.psum(text_share, 'mp')  49.2 us
    psum x1, waiting for transfers between devices, spread(): return lax.psum(kept, axis)  39.1 us
    all_gather x1, waiting for transfers between devices, body(): columns = lax.all_gather(image_low, 'dp', axis=0, tiled=True)  28.6 us
    ppermute x4, waiting for transfers between devices, shifted(): return lax.ppermute(block, axis, route)  27.7 us
    reduce_scatter x1, waiting for transfers between devices, body(): lax.psum_scatter((logit_mult * contract_rows(score_grad, text_low)).astyp...  25.4 us
    reduce_scatter x1, waiting for transfers between devices, body(): lax.psum_scatter(grad_second.astype(jnp.bfloat16), 'dp', scatter_dimensio...  20.6 us
    reduce_scatter x1, waiting for transfers between devices, body(): lax.psum_scatter(grad_first.astype(jnp.bfloat16), 'dp', scatter_dimension...  20.2 us
  transfers between devices with their start and end apart: 15, of which 15 were waited for; matrix products, arithmetic and copies ran while one was open for 6% of the time, Pallas kernels for 0%

commit v1 on v0

--- a/solution.py
+++ b/solution.py
@@ -61,7 +61,12 @@
     image_unit, image_length = unit_rows(image_feats)
     text_low = text_unit.astype(jnp.bfloat16)
     image_low = image_unit.astype(jnp.bfloat16)
-    columns = lax.all_gather(image_low, "dp", axis=0, tiled=True)
+    ring = [image_low]
+    for hop in range(3):
+        ring.append(lax.ppermute(ring[-1], "dp", [(dev, (dev + 1) % 4) for dev in range(4)]))
+    columns = jnp.roll(
+        jnp.concatenate(ring[::-1], axis=0), (lax.axis_index("dp") + 1) * ring[0].shape[0], axis=0
+    )
     column_total_count = columns.shape[0]
     scores = logit_mult * contract_cols(text_low, columns)
     text_ids = dp_index * row_count + jnp.arange(row_count, dtype=jnp.int32)

time: 493 us -> 418 us (0.85)
  waiting for transfers between devices: 358 us -> 282 us
    psum x1, waiting for transfers between devices: 39.1 us -> 0.01 us  [spread(): return lax.psum(kept, axis)]
    all_gather x1 -> x0, waiting for transfers between devices: 28.6 us -> none  [body(): columns = lax.all_gather(image_low, 'dp', axis=0, tiled=True)]
    reduce_scatter x1, waiting for transfers between devices: 25.4 us -> 0.03 us  [body(): lax.psum_scatter((logit_mult * contract_rows(score_grad, text_low)).astyp...]
    ppermute x0 -> x3, waiting for transfers between devices: none -> 23.8 us  [body(): lax.ppermute(ring[-1], 'dp', [(dev, (dev + 1) % 4) for dev in range(4)])]
    reduce_scatter x1, waiting for transfers between devices: 20.2 us -> 14.8 us  [body(): lax.psum_scatter(grad_first.astype(jnp.bfloat16), 'dp', scatter_dimension...]
    unnamed x66 -> x82, local copies, waits for them, and re-layouts: 9.16 us -> 10.5 us
  transfers between devices with their start and end apart: 15 -> 17, of which waited for: 15 -> 15; matrix products, arithmetic and copies ran while one was open for 6% -> 6% of each run, Pallas kernels for 0% -> 0%
where the time goes in v1:
time: 418 us; the launch traced here: 417 us
  waiting for transfers between devices  282 us (67%)
  other arithmetic  39.1 us (9%)
  blocking collectives  30 us (7%)
  matrix products  27.1 us (6%)
  between operations  17.1 us (4%)
  local copies, waits for them, and re-layouts  13.4 us (3%)
  starting transfers between devices  8.83 us (2%)
    psum x5, waiting for transfers between devices, body(): summed = lax.psum(unit_share.astype(jnp.bfloat16), 'mp').astype(jnp.float32)  146 us
    psum x1, waiting for transfers between devices, body(): text_unit_grad = lax.psum(text_share, 'mp')  48.3 us
    ppermute x4, waiting for transfers between devices, shifted(): return lax.ppermute(block, axis, route)  27.8 us
    ppermute x3, waiting for transfers between devices, body(): lax.ppermute(ring[-1], 'dp', [(dev, (dev + 1) % 4) for dev in range(4)])  23.8 us
    reduce_scatter x1, waiting for transfers between devices, body(): lax.psum_scatter(grad_second.astype(jnp.bfloat16), 'dp', scatter_dimensio...  20.5 us
    reduce_scatter x1, waiting for transfers between devices, body(): lax.psum_scatter(grad_first.astype(jnp.bfloat16), 'dp', scatter_dimension...  14.8 us
    dot_general x11, matrix products, contract_rows(): lax.dot_general(left_side, right_side, (((0,), (0,)), ((), ())), preferre...  12.6 us
    unnamed x82, local copies, waits for them, and re-layouts  10.5 us
  transfers between devices with their start and end apart: 17, of which 15 were waited for; matrix products, arithmetic and copies ran while one was open for 6% of the time, Pallas kernels for 0%

profile of v1, /device:TPU:0, one launch (start us, length us, event | category | flops | bytes accessed | tf_op | source)
XLA Modules:
  0.0 417.3 jit_solution(10850209937943559382)
XLA Ops:
  10.3 3.1 collective-permute-start
  13.5 8.3 %collective-permute-done = bf16[256,512]{1,0:T(8,128)(2,1)S(1)} collective-permute-done((bf16[256,512]{1,0:T(8,128)(2,1)S(1)}, bf16[256,512]{1,0:T(8,128)(2,1)S(1)}, u32[]{:S(2)}, u32[]{:S(2)}) %collective-permute-start) | collective-permute-done | bytes 262176 | tf_op jit(solution)/shard_map/ppermute | solution.py:66
  23.3 7.8 %collective-permute-done.1 = bf16[256,512]{1,0:T(8,128)(2,1)S(1)} collective-permute-done((bf16[256,512]{1,0:T(8,128)(2,1)S(1)}, bf16[256,512]{1,0:T(8,128)(2,1)S(1)}, u32[]{:S(2)}, u32[]{:S(2)}) %collective-permute-start.1) | collective-permute-done | bytes 262176 | tf_op jit(solution)/shard_map/ppermute | solution.py:66
  31.8 7.7 %collective-permute-done.2 = bf16[256,512]{1,0:T(8,128)(2,1)S(1)} collective-permute-done((bf16[256,512]{1,0:T(8,128)(2,1)S(1)}, bf16[256,512]{1,0:T(8,128)(2,1)S(1)}, u32[]{:S(2)}, u32[]{:S(2)}) %collective-permute-start.2) | collective-permute-done | bytes 262176 | tf_op jit(solution)/shard_map/ppermute | solution.py:66
  39.9 3.3 multiply_reduce_fusion.1
  43.2 5.6 %pmax.14 = f32[1024]{0:T(1024)S(1)} all-reduce(f32[1024]{0:T(1024)S(1)} %get-tuple-element.14), channel_id=1, replica_groups=mesh['section'=2,'dp'=4,'mp'=4] {'mp'}, use_global_device_ids=true, to_apply=%region_3.4 | all-reduce | flops 1024 | bytes 8192 | tf_op jit(solution)/shard_map/pmax | solution.py:76
  48.8 3.2 fusion
  52.0 8.4 %pmax.15 = f32[1024]{0:T(1024)S(1)} all-reduce(f32[1024]{0:T(1024)S(1)} %get-tuple-element.5), channel_id=1, replica_groups=mesh['section'=2,'dp'=4,'mp'=4] {'dp'}, use_global_device_ids=true, to_apply=%region_7.8 | all-reduce | flops 1024 | bytes 8192 | tf_op jit(solution)/shard_map/pmax | solution.py:77
  63.3 10.4 %psum.64 = f32[1024]{0:T(1024)S(1)} all-reduce(f32[1024]{0:T(1024)S(1)} %fusion.1), channel_id=1, replica_groups=mesh['section'=2,'dp'=4,'mp'=4] {'dp'}, use_global_device_ids=true, to_apply=%region_9.10 | all-reduce | flops 1024 | bytes 8192 | tf_op jit(solution)/shard_map/psum | solution.py:80
  73.7 5.7 %psum.63 = f32[1024]{0:T(1024)S(1)} all-reduce(f32[1024]{0:T(1024)S(1)} %get-tuple-element.4), channel_id=1, replica_groups=mesh['section'=2,'dp'=4,'mp'=4] {'mp'}, use_global_device_ids=true, to_apply=%region_5.6 | all-reduce | flops 1024 | bytes 8192 | tf_op jit(solution)/shard_map/psum | solution.py:78
  79.3 4.0 subtract_convert_fusion
  88.6 48.3 %all-reduce.8.cloned.1.call-done = f32[1024,512]{1,0:T(8,128)} async-done(((f32[1024,512]{1,0:T(8,128)}), f32[1024,512]{1,0:T(8,128)}) %all-reduce.8.cloned.1.call-update) | async-done | bytes 2097168 | tf_op jit(solution)/shard_map/psum | solution.py:85
  142.9 32.5 %all-reduce.10.cloned.1.call-done = bf16[256,512]{1,0:T(8,128)(2,1)} async-done(((bf16[256,512]{1,0:T(8,128)(2,1)}), bf16[256,512]{1,0:T(8,128)(2,1)}) %all-reduce.10.cloned.1.call-update) | async-done | bytes 262160 | tf_op jit(solution)/shard_map/psum | solution.py:119
  179.8 6.8 %collective-permute-done.3 = bf16[256,512]{1,0:T(8,128)(2,1)S(1)} collective-permute-done((bf16[256,512]{1,0:T(8,128)(2,1)S(1)}, bf16[256,512]{1,0:T(8,128)(2,1)S(1)}, u32[]{:S(2)}, u32[]{:S(2)}) %collective-permute-start.3) | collective-permute-done | bytes 262176 | tf_op jit(solution)/shard_map/ppermute | solution.py:12
  189.1 32.4 %all-reduce.12.cloned.1.call-done = bf16[256,512]{1,0:T(8,128)(2,1)} async-done(((bf16[256,512]{1,0:T(8,128)(2,1)}), bf16[256,512]{1,0:T(8,128)(2,1)}) %all-reduce.12.cloned.1.call-update) | async-done | bytes 262160 | tf_op jit(solution)/shard_map/psum | solution.py:119
  225.0 7.1 %collective-permute-done.4 = bf16[256,512]{1,0:T(8,128)(2,1)} collective-permute-done((bf16[256,512]{1,0:T(8,128)(2,1)}, bf16[256,512]{1,0:T(8,128)(2,1)}, u32[]{:S(2)}, u32[]{:S(2)}) %collective-permute-start.4) | collective-permute-done | bytes 262176 | tf_op jit(solution)/shard_map/ppermute | solution.py:12
  235.4 32.4 %all-reduce.14.cloned.1.call-done = bf16[256,512]{1,0:T(8,128)(2,1)} async-done(((bf16[256,512]{1,0:T(8,128)(2,1)}), bf16[256,512]{1,0:T(8,128)(2,1)}) %all-reduce.14.cloned.1.call-update) | async-done | bytes 262160 | tf_op jit(solution)/shard_map/psum | solution.py:119
  271.4 7.1 %collective-permute-done.5 = bf16[256,512]{1,0:T(8,128)(2,1)} collective-permute-done((bf16[256,512]{1,0:T(8,128)(2,1)}, bf16[256,512]{1,0:T(8,128)(2,1)}, u32[]{:S(2)}, u32[]{:S(2)}) %collective-permute-start.5) | collective-permute-done | bytes 262176 | tf_op jit(solution)/shard_map/ppermute | solution.py:12
  282.5 32.4 %all-reduce.16.cloned.1.call-done = bf16[256,512]{1,0:T(8,128)(2,1)} async-done(((bf16[256,512]{1,0:T(8,128)(2,1)}), bf16[256,512]{1,0:T(8,128)(2,1)}) %all-reduce.16.cloned.1.call-update) | async-done | bytes 262160 | tf_op jit(solution)/shard_map/psum | solution.py:119
  318.6 6.9 %collective-permute-done.6 = bf16[256,512]{1,0:T(8,128)(2,1)} collective-permute-done((bf16[256,512]{1,0:T(8,128)(2,1)}, bf16[256,512]{1,0:T(8,128)(2,1)}, u32[]{:S(2)}, u32[]{:S(2)}) %collective-permute-start.6) | collective-permute-done | bytes 262176 | tf_op jit(solution)/shard_map/ppermute | solution.py:12
  329.6 4.0 multiply_convert_fusion
  345.4 16.6 %all-reduce.18.cloned.1.call-done = bf16[256,512]{1,0:T(8,128)(2,1)} async-done(((bf16[256,512]{1,0:T(8,128)(2,1)}), bf16[256,512]{1,0:T(8,128)(2,1)}) %all-reduce.18.cloned.1.call-update) | async-done | bytes 262160 | tf_op jit(solution)/shard_map/psum | solution.py:119
  369.2 14.8 %reduce-scatter.6.cloned.1.call-done = bf16[128,512]{1,0:T(8,128)(2,1)} async-done(((bf16[512,512]{1,0:T(8,128)(2,1)}), bf16[128,512]{1,0:T(8,128)(2,1)}) %reduce-scatter.6.cloned.1.call-update) | async-done | bytes 131088 | tf_op jit(solution)/shard_map/reduce_scatter | solution.py:133
  385.6 20.5 %reduce-scatter.8.cloned.1.call-done = bf16[128,512]{1,0:T(8,128)(2,1)} async-done(((bf16[512,512]{1,0:T(8,128)(2,1)}), bf16[128,512]{1,0:T(8,128)(2,1)}) %reduce-scatter.8.cloned.1.call-update) | async-done | bytes 131088 | tf_op jit(solution)/shard_map/reduce_scatter | solution.py:136
  (163 shorter events, 71.1 us)
Async XLA Ops:
  8.0 79.4 %copy-start = (bf16[1,1024,512]{2,1,0:T(8,128)(2,1)S(1)}, bf16[1,1024,512]{2,1,0:T(8,128)(2,1)}, u32[]{:S(2)}) copy-start(bf16[1,1024,512]{2,1,0:T(8,128)(2,1)} %param.9) | copy-start | bytes 3145732
  8.0 31.5 %copy-start.2 = (bf16[256,512]{1,0:T(8,128)(2,1)S(1)}, bf16[256,512]{1,0:T(8,128)(2,1)}, u32[]{:S(2)}) copy-start(bf16[256,512]{1,0:T(8,128)(2,1)} %param.7) | copy-start | bytes 786436
  8.0 128.9 %all-reduce.8.cloned.1.call-start = ((), (), s32[]{:S(2)}) async-start(), calls=%async_computation.4 | async-start | bytes 4194304 | tf_op jit(solution)/shard_map/psum | solution.py:85
  10.3 11.4 %collective-permute-start = (bf16[256,512]{1,0:T(8,128)(2,1)S(1)}, bf16[256,512]{1,0:T(8,128)(2,1)S(1)}, u32[]{:S(2)}, u32[]{:S(2)}) collective-permute-start(bf16[256,512]{1,0:T(8,128)(2,1)S(1)} %fusion.116), channel_id=1, source_target_pairs={{0,4},{4,8},{8,12},{12,0},{1,5},{5,9},{9,13},{13,1},{2,6},{6,10},{... | collective-permute-start | bytes 786440 | tf_op jit(solution)/shard_map/ppermute | solution.py:66
  21.8 9.3 %collective-permute-start.1 = (bf16[256,512]{1,0:T(8,128)(2,1)S(1)}, bf16[256,512]{1,0:T(8,128)(2,1)S(1)}, u32[]{:S(2)}, u32[]{:S(2)}) collective-permute-start(bf16[256,512]{1,0:T(8,128)(2,1)S(1)} %collective-permute-done), channel_id=1, source_target_pairs={{0,4},{4,8},{8,12},{12,0},{1,5},{5,9},{9,13},{13,1},{2,6},{6,10},{... | collective-permute-start | bytes 786440 | tf_op jit(solution)/shard_map/ppermute | solution.py:66
  31.1 8.4 %collective-permute-start.2 = (bf16[256,512]{1,0:T(8,128)(2,1)S(1)}, bf16[256,512]{1,0:T(8,128)(2,1)S(1)}, u32[]{:S(2)}, u32[]{:S(2)}) collective-permute-start(bf16[256,512]{1,0:T(8,128)(2,1)S(1)} %collective-permute-done.1), channel_id=1, source_target_pairs={{0,4},{4,8},{8,12},{12,0},{1,5},{5,9},{9,13},{13,1},{2,6},{6,10},{... | collective-permute-start | bytes 786440 | tf_op jit(solution)/shard_map/ppermute | solution.py:66
  87.3 88.0 %all-reduce.10.cloned.1.call-start = ((), (), s32[]{:S(2)}) async-start(), calls=%async_computation.5 | async-start | bytes 524288 | tf_op jit(solution)/shard_map/psum | solution.py:119
  88.6 51.1 %copy-start.23 = (f32[256,512]{1,0:T(8,128)}, f32[256,512]{1,0:T(8,128)S(1)}, u32[]{:S(2)}) copy-start(f32[256,512]{1,0:T(8,128)S(1)} %fusion.38) | copy-start | bytes 1572868
  142.8 78.7 %all-reduce.12.cloned.1.call-start = ((), (), s32[]{:S(2)}) async-start(), calls=%async_computation.6 | async-start | bytes 524288 | tf_op jit(solution)/shard_map/psum | solution.py:119
  178.2 8.4 %collective-permute-start.3 = (bf16[256,512]{1,0:T(8,128)(2,1)S(1)}, bf16[256,512]{1,0:T(8,128)(2,1)S(1)}, u32[]{:S(2)}, u32[]{:S(2)}) collective-permute-start(bf16[256,512]{1,0:T(8,128)(2,1)S(1)} %get-tuple-element.13), channel_id=1, source_target_pairs={{16,0},{17,1},{18,2},{19,3},{20,4},{21,5},{22,6},{23,7},{24,8},{25... | collective-permute-start | bytes 786440 | tf_op jit(solution)/shard_map/ppermute | solution.py:12
  187.6 33.9 %copy-start.17 = (bf16[256,512]{1,0:T(8,128)(2,1)}, bf16[256,512]{1,0:T(8,128)(2,1)S(1)}, u32[]{:S(2)}) copy-start(bf16[256,512]{1,0:T(8,128)(2,1)S(1)} %slice_select_fusion.1) | copy-start | bytes 786436
  189.1 78.8 %all-reduce.14.cloned.1.call-start = ((), (), s32[]{:S(2)}) async-start(), calls=%async_computation.7 | async-start | bytes 524288 | tf_op jit(solution)/shard_map/psum | solution.py:119
  223.4 8.7 %collective-permute-start.4 = (bf16[256,512]{1,0:T(8,128)(2,1)}, bf16[256,512]{1,0:T(8,128)(2,1)}, u32[]{:S(2)}, u32[]{:S(2)}) collective-permute-start(bf16[256,512]{1,0:T(8,128)(2,1)} %get-tuple-element.11), channel_id=1, source_target_pairs={{16,0},{17,1},{18,2},{19,3},{20,4},{21,5},{22,6},{23,7},{24,8},{25... | collective-permute-start | bytes 786440 | tf_op jit(solution)/shard_map/ppermute | solution.py:12
  235.4 79.5 %all-reduce.16.cloned.1.call-start = ((), (), s32[]{:S(2)}) async-start(), calls=%async_computation.8 | async-start | bytes 524288 | tf_op jit(solution)/shard_map/psum | solution.py:119
  269.7 8.7 %collective-permute-start.5 = (bf16[256,512]{1,0:T(8,128)(2,1)}, bf16[256,512]{1,0:T(8,128)(2,1)}, u32[]{:S(2)}, u32[]{:S(2)}) collective-permute-start(bf16[256,512]{1,0:T(8,128)(2,1)} %get-tuple-element.9), channel_id=1, source_target_pairs={{16,0},{17,1},{18,2},{19,3},{20,4},{21,5},{22,6},{23,7},{24,8},{25... | collective-permute-start | bytes 786440 | tf_op jit(solution)/shard_map/ppermute | solution.py:12
  271.0 9.2 %copy-start.36 = (bf16[1,512,512]{2,1,0:T(8,128)(2,1)S(1)}, bf16[1,512,512]{2,1,0:T(8,128)(2,1)}, u32[]{:S(2)}) copy-start(bf16[1,512,512]{2,1,0:T(8,128)(2,1)} %param.11) | copy-start | bytes 1572868
  271.3 9.3 %copy-start.27 = (f32[256,512]{1,0:T(8,128)}, f32[256,512]{1,0:T(8,128)S(1)}, u32[]{:S(2)}) copy-start(f32[256,512]{1,0:T(8,128)S(1)} %fusion.29) | copy-start | bytes 1572868
  282.4 79.5 %all-reduce.18.cloned.1.call-start = ((), (), s32[]{:S(2)}) async-start(), calls=%async_computation.9 | async-start | bytes 524288 | tf_op jit(solution)/shard_map/psum | solution.py:119
  316.8 8.7 %collective-permute-start.6 = (bf16[256,512]{1,0:T(8,128)(2,1)}, bf16[256,512]{1,0:T(8,128)(2,1)}, u32[]{:S(2)}, u32[]{:S(2)}) collective-permute-start(bf16[256,512]{1,0:T(8,128)(2,1)} %get-tuple-element.7), channel_id=1, source_target_pairs={{16,0},{17,1},{18,2},{19,3},{20,4},{21,5},{22,6},{23,7},{24,8},{25... | collective-permute-start | bytes 786440 | tf_op jit(solution)/shard_map/ppermute | solution.py:12
  318.6 9.1 %copy-start.29 = (f32[256,512]{1,0:T(8,128)}, f32[256,512]{1,0:T(8,128)S(1)}, u32[]{:S(2)}) copy-start(f32[256,512]{1,0:T(8,128)S(1)} %fusion.26) | copy-start | bytes 1572868
  329.5 36.6 %reduce-scatter.4.cloned.1.call-start = ((), (), s32[]{:S(2)}) async-start(), calls=%async_computation.3 | async-start | bytes 1310720 | tf_op jit(solution)/shard_map/reduce_scatter | solution.py:87
  333.6 50.4 %reduce-scatter.6.cloned.1.call-start = ((), (), s32[]{:S(2)}) async-start(), calls=%async_computation.11 | async-start | bytes 655360 | tf_op jit(solution)/shard_map/reduce_scatter | solution.py:133
  340.0 66.1 %reduce-scatter.8.cloned.1.call-start = ((), (), s32[]{:S(2)}) async-start(), calls=%async_computation.12 | async-start | bytes 655360 | tf_op jit(solution)/shard_map/reduce_scatter | solution.py:136
  345.3 62.5 %all-reduce.20.cloned.1.call-start = ((), (), s32[]{:S(2)}) async-start(), calls=%async_computation.10 | async-start | bytes 2097152 | tf_op jit(solution)/shard_map/psum | solution.py:17
  (31 other events, 89.2 us)
Sparse Core Ops, SparseCore 0:
  87.4 49.4 all-reduce.7
  142.9 32.3 all-reduce.9
  189.2 32.2 all-reduce.11
  235.5 32.2 all-reduce.13
  282.5 32.2 all-reduce.15
  329.6 32.2 all-reduce.17
  366.2 39.1 all-reduce.19
Sparse Core Ops, SparseCore 1:
  333.7 27.2 reduce-scatter.3
  363.6 20.3 reduce-scatter.5
  386.2 19.9 reduce-scatter.7
